TPU v7x, 32 devices: a whole 2x2x4 slice. The times are simulated.
32 devices in a mesh: gy: 8 (over y, x, core), gx: 4 (over z).
Axes of the slice: x: 2, y: 2, z: 4, core: 2. Of those that a mesh axis runs over, the one named last changes fastest.
Arguments:
- left_factor: bfloat16 [8192, 2048], P('gy', 'gx'), may hold values from -6 to 6
- right_factor: bfloat16 [2048, 8192], P('gy', 'gx'), may hold values from -0.125 to 0.125
Outputs:
- corrected: float32 [8192, 8192], P('gy', 'gx')
All inputs are finite; a program needn't handle non-finite values.
Results may differ from a plain program's by a relative error of at most 0.0003.
Values may be sent and summed in bfloat16 or wider, within the bound.
A program may use at most 192 MiB of HBM per device.

v0:
```python
import jax
import jax.numpy as jnp
from jax import lax
from jax.sharding import PartitionSpec as P


def absorb_panel(left_panel, right_panel):
    return jnp.dot(left_panel, right_panel, preferred_element_type=jnp.float32)


def per_device(left_factor, right_factor):
    right_line = lax.all_gather(right_factor, "gy", axis=0, tiled=True)
    total = absorb_panel(lax.all_gather(left_factor, "gx", axis=1, tiled=True), right_line)
    corrected = total
    row_power = lax.psum(jnp.sum(corrected * corrected, axis=1), "gx")
    corrected = (
        corrected
        * lax.rsqrt(row_power / (corrected.shape[1] * lax.axis_size("gx")) + 1e-06)[:, None]
    )
    return corrected


def solution(mesh):
    placed = (P("gy", "gx"), P("gy", "gx"))
    return jax.shard_map(
        per_device, mesh=mesh, in_specs=placed, out_specs=P("gy", "gx"), check_vma=False
    )
```

profile of v0, /device:TPU:0, one launch (start us, length us, event | category | flops | bytes accessed | tf_op | source)
XLA Modules:
  0.0 187.5 jit_solution(11503262630804149918)
XLA Ops:
  6.5 0.0 all-gather.3.cloned.1.call-start
  6.5 0.7 all-gather.3.cloned.1.call-update
  7.3 0.0 all-gather.5.cloned.1.call-start
  7.3 0.7 all-gather.5.cloned.1.call-update
  8.0 84.4 %all-gather.3.cloned.1.call-done = bf16[1024,2048]{1,0:T(8,128)(2,1)} async-done(((bf16[1024,512]{1,0:T(8,128)(2,1)}), bf16[1024,2048]{1,0:T(8,128)(2,1)}) %all-gather.3.cloned.1.call-update) | async-done | bytes 4194320 | tf_op jit(solution)/shard_map/all_gather | solution.py:13
  92.4 54.7 %all-gather.5.cloned.1.call-done = bf16[2048,2048]{1,0:T(8,128)(2,1)} async-done(((bf16[256,2048]{1,0:T(8,128)(2,1)}), bf16[2048,2048]{1,0:T(8,128)(2,1)}) %all-gather.5.cloned.1.call-update) | async-done | bytes 8388624 | tf_op jit(solution)/shard_map/all_gather | solution.py:12
  147.1 14.5 %multiply_reduce_fusion = (f32[1024]{0:T(1024)S(1)}, f32[1024,2048]{1,0:T(8,128)}) fusion(bf16[1024,2048]{1,0:T(8,128)(2,1)} %all-gather.3.cloned.1.call-done, bf16[2048,2048]{1,0:T(8,128)(2,1)} %all-gather.5.cloned.1.call-done), kind=kOutput, calls=%fused_computation | convolution fusion | flops 8594127872 | bytes 20975616 | tf_op jit(solution)/shard_map/dot_general | solution.py:8
  161.6 11.7 %psum.7 = f32[1024]{0:T(1024)S(1)} all-reduce(f32[1024]{0:T(1024)S(1)} %get-tuple-element.5), channel_id=1, replica_groups=mesh['gy'=8,'gx'=4] {'gx'}, use_global_device_ids=true, to_apply=%region_1.0 | all-reduce | flops 1024 | bytes 8192 | tf_op jit(solution)/shard_map/psum | solution.py:15
  173.3 7.4 %broadcast_multiply_fusion = f32[1024,2048]{1,0:T(8,128)} fusion(f32[1024,2048]{1,0:T(8,128)} %get-tuple-element.6, f32[1024]{0:T(1024)S(1)} %add_rsqrt_fusion), kind=kLoop, calls=%fused_computation.1 | loop fusion | flops 2097152 | bytes 16781312 | tf_op jit(solution)/shard_map/mul | solution.py:17
  (1 shorter events, 0.0 us)
Async XLA Ops:
  6.5 85.9 %all-gather.3.cloned.1.call-start = ((), (), s32[]{:S(2)}) async-start(), calls=%async_computation | async-start | bytes 5242880 | tf_op jit(solution)/shard_map/all_gather | solution.py:13
  7.3 139.8 %all-gather.5.cloned.1.call-start = ((), (), s32[]{:S(2)}) async-start(), calls=%async_computation.1 | async-start | bytes 9437184 | tf_op jit(solution)/shard_map/all_gather | solution.py:12
Sparse Core Ops, SparseCore 0:
  8.9 83.4 all-gather.2
  94.3 52.7 all-gather.4
where the time goes:
time: 188 us
  waiting for transfers between devices  140 us (74%)
  matrix products  14.5 us (8%)
  between operations  13.4 us (7%)
  blocking collectives  11.7 us (6%)
  other arithmetic  7.4 us (4%)
    all_gather x1, waiting for transfers between devices, per_device(): lax.all_gather(left_factor, 'gx', axis=1, tiled=True)  84.4 us
    all_gather x1, waiting for transfers between devices, per_device(): right_line = lax.all_gather(right_factor, 'gy', axis=0, tiled=True)  54.7 us
    dot_general x1, matrix products, absorb_panel(): return jnp.dot(left_panel, right_panel, preferred_element_type=jnp.float32)  14.5 us
    psum x1, blocking collectives, per_device(): row_power = lax.psum(jnp.sum(corrected * corrected, axis=1), 'gx')  11.7 us
    mul x1, other arithmetic, per_device(): corrected * lax.rsqrt(row_power / (corrected.shape[1] * lax.axis_size('gx...  7.39 us
  transfers between devices with their start and end apart: 2, of which 2 were waited for; matrix products, arithmetic and copies ran while one was open for 0% of the time, Pallas kernels for 0%

commit v1 on v0

v1 whole, which is shorter than its diff:
```python
import functools

import jax
import jax.numpy as jnp
from jax import lax
from jax.experimental import pallas as pl
from jax.experimental.pallas import tpu as pltpu
from jax.sharding import PartitionSpec as P

MESH = pl.DeviceIdType.MESH
CHUNK = 128
CORES = 2


def other_chip(chip, offset, chips):
    if chips & (chips - 1):
        return (chip + offset) % chips
    for bit in range(chips.bit_length() - 1):
        if (offset >> bit) & 1:
            chip = chip + (1 << bit) * (1 - 2 * ((chip // (1 << bit)) % 2))
    return chip


def kernel(m, n, left, right, acc, scale, a, b, power, own_sem, a_send, a_recv, b_send, b_pass, b_recv, p_send, p_recv):
    gy, gx = lax.axis_index("gy"), lax.axis_index("gx")
    rows, ka = left.shape
    kb, cols = right.shape
    chunks, chips = rows // CHUNK, m // CORES
    chip, core = gy // CORES, gy % CORES
    partner = chip * CORES + (1 - core)
    has_right, has_left = gx < n - 1, gx > 0

    def peer(offset, which):
        return other_chip(chip, offset, chips) * CORES + which

    barrier = pltpu.get_barrier_semaphore()
    greeted = [(peer(p, core), gx) for p in range(1, chips)] + [(partner, gx)]
    greeted += [(gy, (gx + d) % n) for d in range(1, n)]
    for device in greeted:
        pl.semaphore_signal(barrier, inc=1, device_id=device, device_id_type=MESH)
    pl.semaphore_wait(barrier, len(greeted))

    def a_slot(block, r):
        return a.at[
            pl.ds(pl.multiple_of(r * CHUNK, CHUNK), CHUNK),
            pl.ds(pl.multiple_of(block * ka, ka), ka),
        ]

    def a_copy(block, r, way, source=None):
        return pltpu.make_async_remote_copy(
            src_ref=a_slot(block, r) if source is None else source,
            dst_ref=a_slot(block, r),
            send_sem=a_send.at[way, block, r],
            recv_sem=a_recv.at[block, r],
            device_id=(gy, gx + 2 * way - 1),
            device_id_type=MESH,
        )

    def own_a(r, way):
        return a_copy(gx, r, way, left.at[pl.ds(pl.multiple_of(r * CHUNK, CHUNK), CHUNK), :])

    def b_slot(block):
        return b.at[pl.ds(pl.multiple_of(block * kb, kb), kb), :]

    def b_copy(p):
        return pltpu.make_async_remote_copy(
            src_ref=right,
            dst_ref=b_slot(gy),
            send_sem=b_send.at[p],
            recv_sem=b_recv.at[gy],
            device_id=(partner, gx) if p == 0 else (peer(p, core), gx),
            device_id_type=MESH,
        )

    def b_onward(p):
        block = peer(p, core)
        return pltpu.make_async_remote_copy(
            src_ref=b_slot(block),
            dst_ref=b_slot(block),
            send_sem=b_pass.at[p],
            recv_sem=b_recv.at[block],
            device_id=(partner, gx),
            device_id_type=MESH,
        )

    def b_arrival(block):
        return pltpu.make_async_remote_copy(
            src_ref=b_slot(block),
            dst_ref=b_slot(block),
            send_sem=b_pass.at[0],
            recv_sem=b_recv.at[block],
            device_id=(partner, gx),
            device_id_type=MESH,
        )

    def each_chunk(body):
        lax.fori_loop(0, chunks, lambda r, carry: (body(r), carry)[1], 0)

    @each_chunk
    def _(r):
        @pl.when(has_right)
        def _():
            own_a(r, 1).start()

        @pl.when(has_left)
        def _():
            own_a(r, 0).start()

    for p in [*range(1, chips), 0]:
        b_copy(p).start()
    keep_a = pltpu.make_async_copy(left, a.at[:, pl.ds(pl.multiple_of(gx * ka, ka), ka)], own_sem.at[0])
    keep_b = pltpu.make_async_copy(right, b_slot(gy), own_sem.at[1])
    keep_a.start()
    keep_b.start()

    def pass_b(p):
        b_arrival(peer(p, core)).wait_recv()
        b_onward(p).start()

    def relay(d, r, act):
        @pl.when(jnp.logical_and(gx >= d, has_right))
        def _():
            act(gx - d, r, 1)

        @pl.when(jnp.logical_and(gx + d < n, has_left))
        def _():
            act(gx + d, r, 0)

    def receive_and_pass(block, r, way):
        a_copy(block, r, way).wait_recv()
        a_copy(block, r, way).start()

    early = max(chips - 2, 0)
    for d in range(1, n - 1):
        each_chunk(lambda r: relay(d, r, receive_and_pass))
        if d == 1:
            for p in range(1, 1 + early):
                pass_b(p)
    for p in range(1 + (early if n > 2 else 0), chips):
        pass_b(p)

    keep_a.wait()
    keep_b.wait()
    at_end = jnp.logical_or(gx == 0, gx == n - 1)
    for block in range(1, n - 1):

        @each_chunk
        def _(r):
            @pl.when(at_end)
            def _():
                a_copy(block, r, 0).wait_recv()

    for p in range(chips):
        b_arrival(peer(p, 1 - core)).wait_recv()

    upper = (2 * gx) // n
    far = (n - 1) * (1 - upper)
    near_k = (n - 1) * ka
    near = pl.ds(pl.multiple_of(upper * ka, ka), near_k)
    far_k = pl.ds(pl.multiple_of(far * ka, ka), ka)
    wide = 512 if cols % 512 == 0 else cols
    tall = 256 if rows % 256 == 0 else CHUNK

    def near_tile(i, carry):
        tile_rows = pl.ds(pl.multiple_of((i // (cols // wide)) * tall, tall), tall)
        tile_cols = pl.ds(pl.multiple_of((i % (cols // wide)) * wide, wide), wide)
        acc[tile_rows, tile_cols] = jnp.dot(
            a[tile_rows, near], b[near, tile_cols], preferred_element_type=jnp.float32
        )
        return carry

    lax.fori_loop(0, (rows // tall) * (cols // wide), near_tile, 0)

    @each_chunk
    def _(r):
        @pl.when(at_end)
        def _():
            a_copy(far, r, 0).wait_recv()

        here = pl.ds(pl.multiple_of(r * CHUNK, CHUNK), CHUNK)
        squares = jnp.zeros((CHUNK, 128), jnp.float32)
        for c in range(0, cols, wide):
            tile = acc[here, c : c + wide] + jnp.dot(
                a[here, far_k], b[far_k, c : c + wide], preferred_element_type=jnp.float32
            )
            acc[here, c : c + wide] = tile
            for lane in range(0, wide, 128):
                squares = squares + tile[:, lane : lane + 128] * tile[:, lane : lane + 128]
        power[gx, pl.ds(r, 1), :] = jnp.sum(squares.T, axis=0, keepdims=True)

    def p_copy(d, block):
        return pltpu.make_async_remote_copy(
            src_ref=power.at[block],
            dst_ref=power.at[block],
            send_sem=p_send.at[d],
            recv_sem=p_recv.at[block],
            device_id=(gy, (gx + d) % n),
            device_id_type=MESH,
        )

    for d in range(1, n):
        p_copy(d, gx).start()

    @each_chunk
    def _(r):
        @pl.when(has_right)
        def _():
            own_a(r, 1).wait_send()

        @pl.when(has_left)
        def _():
            own_a(r, 0).wait_send()

        for d in range(1, n - 1):
            relay(d, r, lambda block, r, way: a_copy(block, r, way).wait_send())

    for p in range(chips):
        b_copy(p).wait_send()
        if p:
            b_onward(p).wait_send()
    for d in range(1, n):
        p_copy(d, (gx + d) % n).wait_recv()
    total = power[0]
    for z in range(1, n):
        total = total + power[z]
    scale[...] = lax.rsqrt(total / (cols * n) + 1e-06)
    for d in range(1, n):
        p_copy(d, gx).wait_send()


def per_device(m, n, left_factor, right_factor):
    rows, ka = left_factor.shape
    kb, cols = right_factor.shape
    chunks, chips = rows // CHUNK, m // CORES
    dma = pltpu.SemaphoreType.DMA
    product, scale = pl.pallas_call(
        functools.partial(kernel, m, n),
        out_shape=[
            pltpu.VMEM((rows, cols), jnp.float32),
            jax.ShapeDtypeStruct((chunks, 128), jnp.float32),
        ],
        in_specs=[pl.BlockSpec(memory_space=pl.ANY)] * 2,
        out_specs=[pl.BlockSpec(memory_space=pltpu.VMEM)] * 2,
        scratch_shapes=[
            pltpu.VMEM((rows, n * ka), left_factor.dtype),
            pltpu.VMEM((m * kb, cols), right_factor.dtype),
            pltpu.VMEM((n, chunks, 128), jnp.float32),
            dma((2,)),
            dma((2, n, chunks)),
            dma((n, chunks)),
            dma((chips,)),
            dma((chips,)),
            dma((m,)),
            dma((n,)),
            dma((n,)),
        ],
        compiler_params=pltpu.CompilerParams(
            collective_id=0,
            has_side_effects=True,
            vmem_limit_bytes=n * ka * rows * 2 + m * kb * cols * 2 + 5 * 2**20,
        ),
    )(left_factor, right_factor)
    return product * scale.reshape(rows)[:, None]


def solution(mesh):
    placed = (P("gy", "gx"), P("gy", "gx"))
    return jax.shard_map(
        functools.partial(per_device, mesh.shape["gy"], mesh.shape["gx"]),
        mesh=mesh,
        in_specs=placed,
        out_specs=P("gy", "gx"),
        check_vma=False,
    )
```

time: 188 us -> 85.8 us (0.46)
  waiting for transfers between devices: 140 us -> 0 us
  Pallas kernels: 0 us -> 79.2 us
  matrix products: 14.5 us -> 0 us
  between operations: 13.4 us -> 0.01 us
  blocking collectives: 11.7 us -> 0 us
  other arithmetic: 7.4 us -> 4.01 us
  local copies, waits for them, and re-layouts: 0 us -> 2.45 us
    all_gather x2 -> x0, waiting for transfers between devices: 139 us -> none  [the longest x1 84.4 us: per_device(): lax.all_gather(left_factor, 'gx', axis=1, tiled=True)]
    pallas_call x0 -> x1, Pallas kernels: none -> 79.2 us  [per_device(): pl.pallas_call(functools.partial(kernel, m, n), out_shape=[pltpu.VMEM((ro...]
    dot_general x1 -> x0, matrix products: 14.5 us -> none  [absorb_panel(): return jnp.dot(left_panel, right_panel, preferred_element_type=jnp.float32)]
    psum x1 -> x0, blocking collectives: 11.7 us -> none  [per_device(): row_power = lax.psum(jnp.sum(corrected * corrected, axis=1), 'gx')]
    mul x1, other arithmetic: 7.39 us -> 4.01 us  [per_device(): return product * scale.reshape(rows)[:, None]]
    unnamed x0 -> x4, local copies, waits for them, and re-layouts: none -> 2.45 us
  transfers between devices with their start and end apart: 2 -> 0, of which waited for: 2 -> 0; matrix products, arithmetic and copies ran while one was open for 0% -> 0% of each run, Pallas kernels for 0% -> 0%
where the time goes in v1:
time: 85.8 us; the launch traced here: 85.6 us
  Pallas kernels  79.2 us (92%)
  other arithmetic  4.01 us (5%)
  local copies, waits for them, and re-layouts  2.45 us (3%)
    pallas_call x1, Pallas kernels, per_device(): pl.pallas_call(functools.partial(kernel, m, n), out_shape=[pltpu.VMEM((ro...  79.2 us
    mul x1, other arithmetic, per_device(): return product * scale.reshape(rows)[:, None]  4.01 us
    unnamed x4, local copies, waits for them, and re-layouts  2.45 us

profile of v1, /device:TPU:0, one launch (start us, length us, event | category | flops | bytes accessed | tf_op | source)
XLA Modules:
  0.0 85.6 jit_solution(6575640621120723926)
XLA Ops:
  0.0 0.0 copy-start
  0.0 1.2 %copy-done = bf16[1024,512]{1,0:T(8,128)(2,1)S(1)} copy-done((bf16[1024,512]{1,0:T(8,128)(2,1)S(1)}, bf16[1024,512]{1,0:T(8,128)(2,1)}, u32[]{:S(2)}) %copy-start) | copy-done | bytes 1048600
  1.2 0.0 copy-start.1
  1.2 1.2 %copy-done.1 = bf16[256,2048]{1,0:T(8,128)(2,1)S(1)} copy-done((bf16[256,2048]{1,0:T(8,128)(2,1)S(1)}, bf16[256,2048]{1,0:T(8,128)(2,1)}, u32[]{:S(2)}) %copy-start.1) | copy-done | bytes 1048600
  2.5 79.2 %shard_map.28 = (f32[1024,2048]{1,0:T(8,128)S(1)}, f32[8,128]{1,0:T(8,128)S(1)}) custom-call(bf16[1024,512]{1,0:T(8,128)(2,1)S(1)} %copy-done, bf16[256,2048]{1,0:T(8,128)(2,1)S(1)} %copy-done.1), custom_call_target="tpu_custom_call" | custom-call | tf_op jit(solution)/shard_map/pallas_call | solution.py:236
  81.6 4.0 %broadcast_multiply_fusion = f32[1024,2048]{1,0:T(8,128)} fusion(f32[1024,2048]{1,0:T(8,128)S(1)} %get-tuple-element.7, f32[1024]{0:T(1024)S(1)} %bitcast.1), kind=kLoop, calls=%fused_computation | loop fusion | flops 2097152 | bytes 16781312 | tf_op jit(solution)/shard_map/mul | solution.py:263
Async XLA Ops:
  0.0 1.2 %copy-start = (bf16[1024,512]{1,0:T(8,128)(2,1)S(1)}, bf16[1024,512]{1,0:T(8,128)(2,1)}, u32[]{:S(2)}) copy-start(bf16[1024,512]{1,0:T(8,128)(2,1)} %left.1) | copy-start | bytes 3145732
  1.2 1.2 %copy-start.1 = (bf16[256,2048]{1,0:T(8,128)(2,1)S(1)}, bf16[256,2048]{1,0:T(8,128)(2,1)}, u32[]{:S(2)}) copy-start(bf16[256,2048]{1,0:T(8,128)(2,1)} %right.1) | copy-start | bytes 3145732

commit v2 on v1

--- a/solution.py
+++ b/solution.py
@@ -10,6 +10,7 @@
 MESH = pl.DeviceIdType.MESH
 CHUNK = 128
 CORES = 2
+VMEM_BYTES = 67043328
 
 
 def other_chip(chip, offset, chips):
@@ -228,6 +229,26 @@
         p_copy(d, gx).wait_send()
 
 
+def finish(product, scale, out, staged, sem):
+    rows, cols = product.shape
+
+    def copy(r):
+        here = pl.ds(pl.multiple_of(r * CHUNK, CHUNK), CHUNK)
+        return pltpu.make_async_copy(staged.at[here], out.at[here], sem.at[r])
+
+    def scale_chunk(r, carry):
+        here = pl.ds(pl.multiple_of(r * CHUNK, CHUNK), CHUNK)
+        by_row = jnp.broadcast_to(scale[pl.ds(r, 1), :], (CHUNK, CHUNK)).T
+        for lane in range(0, cols, CHUNK):
+            staged[here, lane : lane + CHUNK] = product[here, lane : lane + CHUNK] * by_row
+        copy(r).start()
+        return carry
+
+    lax.fori_loop(0, rows // CHUNK, scale_chunk, 0)
+    for r in range(rows // CHUNK):
+        copy(r).wait()
+
+
 def per_device(m, n, left_factor, right_factor):
     rows, ka = left_factor.shape
     kb, cols = right_factor.shape
@@ -237,9 +258,9 @@
         functools.partial(kernel, m, n),
         out_shape=[
             pltpu.VMEM((rows, cols), jnp.float32),
-            jax.ShapeDtypeStruct((chunks, 128), jnp.float32),
+            pltpu.VMEM((chunks, 128), jnp.float32),
         ],
-        in_specs=[pl.BlockSpec(memory_space=pl.ANY)] * 2,
+        in_specs=[pl.BlockSpec(memory_space=pltpu.HBM)] * 2,
         out_specs=[pl.BlockSpec(memory_space=pltpu.VMEM)] * 2,
         scratch_shapes=[
             pltpu.VMEM((rows, n * ka), left_factor.dtype),
@@ -257,10 +278,17 @@
         compiler_params=pltpu.CompilerParams(
             collective_id=0,
             has_side_effects=True,
-            vmem_limit_bytes=n * ka * rows * 2 + m * kb * cols * 2 + 5 * 2**20,
+            vmem_limit_bytes=VMEM_BYTES - rows * cols * 4 - 2**19,
         ),
     )(left_factor, right_factor)
-    return product * scale.reshape(rows)[:, None]
+    return pl.pallas_call(
+        finish,
+        out_shape=jax.ShapeDtypeStruct((rows, cols), jnp.float32),
+        in_specs=[pl.BlockSpec(memory_space=pltpu.VMEM)] * 2,
+        out_specs=pl.BlockSpec(memory_space=pl.ANY),
+        scratch_shapes=[pltpu.VMEM((rows, cols), jnp.float32), dma((chunks,))],
+        compiler_params=pltpu.CompilerParams(vmem_limit_bytes=rows * cols * 4 + 2 * 2**20),
+    )(product, scale)
 
 
 def solution(mesh):

time: 85.8 us -> 83 us (0.967)
  other arithmetic: 4.01 us -> 0 us
  Pallas kernels: 79.2 us -> 82.9 us
  local copies, waits for them, and re-layouts: 2.45 us -> 0 us
    mul x1 -> x0, other arithmetic: 4.01 us -> none  [per_device(): return product * scale.reshape(rows)[:, None]]
    pallas_call x0 -> x1, Pallas kernels: none -> 3.5 us  [per_device(): pl.pallas_call(finish, out_shape=jax.ShapeDtypeStruct((rows, cols), jnp.f...]
    unnamed x4 -> x0, local copies, waits for them, and re-layouts: 2.45 us -> none
where the time goes in v2:
time: 83 us; the launch traced here: 82.9 us
  Pallas kernels  82.9 us (100%)
    pallas_call x1, Pallas kernels, per_device(): pl.pallas_call(functools.partial(kernel, m, n), out_shape=[pltpu.VMEM((ro...  79.4 us
    pallas_call x1, Pallas kernels, per_device(): pl.pallas_call(finish, out_shape=jax.ShapeDtypeStruct((rows, cols), jnp.f...  3.5 us

profile of v2, /device:TPU:0, one launch (start us, length us, event | category | flops | bytes accessed | tf_op | source)
XLA Modules:
  0.0 82.9 jit_solution(13501907833407963178)
XLA Ops:
  0.0 79.4 %shard_map.28 = (f32[1024,2048]{1,0:T(8,128)S(1)}, f32[8,128]{1,0:T(8,128)S(1)}) custom-call(bf16[1024,512]{1,0:T(8,128)(2,1)} %left.1, bf16[256,2048]{1,0:T(8,128)(2,1)} %right.1), custom_call_target="tpu_custom_call" | custom-call | tf_op jit(solution)/shard_map/pallas_call | solution.py:257
  79.4 3.5 %shard_map.29 = f32[1024,2048]{1,0:T(8,128)} custom-call(f32[1024,2048]{1,0:T(8,128)S(1)} %get-tuple-element.7.product, f32[8,128]{1,0:T(8,128)S(1)} %get-tuple-element.8.scale), custom_call_target="tpu_custom_call" | custom-call | tf_op jit(solution)/shard_map/pallas_call | solution.py:284

commit v3 on v2

--- a/solution.py
+++ b/solution.py
@@ -10,6 +10,7 @@
 MESH = pl.DeviceIdType.MESH
 CHUNK = 128
 CORES = 2
+TAIL = 2
 VMEM_BYTES = 67043328
 
 
@@ -22,7 +23,7 @@
     return chip
 
 
-def kernel(m, n, left, right, acc, scale, a, b, power, own_sem, a_send, a_recv, b_send, b_pass, b_recv, p_send, p_recv):
+def kernel(m, n, left, right, acc, scale, a, b, power, tail_power, early_scale, own_sem, a_send, a_recv, b_send, b_pass, b_recv, p_send, p_recv):
     gy, gx = lax.axis_index("gy"), lax.axis_index("gx")
     rows, ka = left.shape
     kb, cols = right.shape
@@ -172,8 +173,7 @@
 
     lax.fori_loop(0, (rows // tall) * (cols // wide), near_tile, 0)
 
-    @each_chunk
-    def _(r):
+    def far_chunk(r):
         @pl.when(at_end)
         def _():
             a_copy(far, r, 0).wait_recv()
@@ -187,20 +187,53 @@
             acc[here, c : c + wide] = tile
             for lane in range(0, wide, 128):
                 squares = squares + tile[:, lane : lane + 128] * tile[:, lane : lane + 128]
-        power[gx, pl.ds(r, 1), :] = jnp.sum(squares.T, axis=0, keepdims=True)
-
-    def p_copy(d, block):
-        return pltpu.make_async_remote_copy(
-            src_ref=power.at[block],
-            dst_ref=power.at[block],
-            send_sem=p_send.at[d],
-            recv_sem=p_recv.at[block],
+        return jnp.sum(squares.T, axis=0, keepdims=True)
+
+    def early_chunk(r, carry):
+        power[gx, pl.ds(r, 1), :] = far_chunk(r)
+        return carry
+
+    def share(which, block, d):
+        part = (power, tail_power)[which].at[block]
+        return pltpu.make_async_remote_copy(
+            src_ref=part,
+            dst_ref=part,
+            send_sem=p_send.at[which, d],
+            recv_sem=p_recv.at[which, block],
             device_id=(gy, (gx + d) % n),
             device_id_type=MESH,
         )
 
+    def gathered(which):
+        sums = (power, tail_power)[which]
+        for d in range(1, n):
+            share(which, (gx + d) % n, d).wait_recv()
+        total = sums[0]
+        for z in range(1, n):
+            total = total + sums[z]
+        return lax.rsqrt(total / (cols * n) + 1e-06)
+
+    first = chunks - TAIL
+    power[gx] = jnp.zeros((chunks, 128), jnp.float32)
+    tail_power[gx] = jnp.zeros((8, 128), jnp.float32)
+    lax.fori_loop(0, first, early_chunk, 0)
     for d in range(1, n):
-        p_copy(d, gx).start()
+        share(0, gx, d).start()
+    for r in range(TAIL):
+        tail_power[gx, pl.ds(r, 1), :] = far_chunk(first + r)
+    for d in range(1, n):
+        share(1, gx, d).start()
+
+    early_scale[...] = gathered(0)
+
+    def scale_chunk(r, carry):
+        here = pl.ds(pl.multiple_of(r * CHUNK, CHUNK), CHUNK)
+        factor = by_row(early_scale[pl.ds(r, 1), :])
+        for lane in range(0, cols, CHUNK):
+            acc[here, lane : lane + CHUNK] = acc[here, lane : lane + CHUNK] * factor
+        return carry
+
+    lax.fori_loop(0, first, scale_chunk, 0)
 
     @each_chunk
     def _(r):
@@ -220,32 +253,35 @@
         if p:
             b_onward(p).wait_send()
     for d in range(1, n):
-        p_copy(d, (gx + d) % n).wait_recv()
-    total = power[0]
-    for z in range(1, n):
-        total = total + power[z]
-    scale[...] = lax.rsqrt(total / (cols * n) + 1e-06)
-    for d in range(1, n):
-        p_copy(d, gx).wait_send()
+        share(0, gx, d).wait_send()
+        share(1, gx, d).wait_send()
+    scale[...] = gathered(1)
+
+
+def by_row(sums):
+    return jnp.broadcast_to(sums, (CHUNK, CHUNK)).T
 
 
 def finish(product, scale, out, staged, sem):
     rows, cols = product.shape
+    chunks = rows // CHUNK
+    first = chunks - TAIL
 
     def copy(r):
-        here = pl.ds(pl.multiple_of(r * CHUNK, CHUNK), CHUNK)
-        return pltpu.make_async_copy(staged.at[here], out.at[here], sem.at[r])
-
-    def scale_chunk(r, carry):
-        here = pl.ds(pl.multiple_of(r * CHUNK, CHUNK), CHUNK)
-        by_row = jnp.broadcast_to(scale[pl.ds(r, 1), :], (CHUNK, CHUNK)).T
+        here = pl.ds(r * CHUNK, CHUNK)
+        source = product.at[here] if r < first else staged.at[r - first]
+        return pltpu.make_async_copy(source, out.at[here], sem.at[r])
+
+    for r in range(first):
+        copy(r).start()
+    for r in range(first, chunks):
+        factor = by_row(scale[r - first : r - first + 1, :])
         for lane in range(0, cols, CHUNK):
-            staged[here, lane : lane + CHUNK] = product[here, lane : lane + CHUNK] * by_row
+            staged[r - first, :, lane : lane + CHUNK] = (
+                product[r * CHUNK : (r + 1) * CHUNK, lane : lane + CHUNK] * factor
+            )
         copy(r).start()
-        return carry
-
-    lax.fori_loop(0, rows // CHUNK, scale_chunk, 0)
-    for r in range(rows // CHUNK):
+    for r in range(chunks):
         copy(r).wait()
 
 
@@ -258,7 +294,7 @@
         functools.partial(kernel, m, n),
         out_shape=[
             pltpu.VMEM((rows, cols), jnp.float32),
-            pltpu.VMEM((chunks, 128), jnp.float32),
+            pltpu.VMEM((8, 128), jnp.float32),
         ],
         in_specs=[pl.BlockSpec(memory_space=pltpu.HBM)] * 2,
         out_specs=[pl.BlockSpec(memory_space=pltpu.VMEM)] * 2,
@@ -266,14 +302,16 @@
             pltpu.VMEM((rows, n * ka), left_factor.dtype),
             pltpu.VMEM((m * kb, cols), right_factor.dtype),
             pltpu.VMEM((n, chunks, 128), jnp.float32),
+            pltpu.VMEM((n, 8, 128), jnp.float32),
+            pltpu.VMEM((chunks, 128), jnp.float32),
             dma((2,)),
             dma((2, n, chunks)),
             dma((n, chunks)),
             dma((chips,)),
             dma((chips,)),
             dma((m,)),
-            dma((n,)),
-            dma((n,)),
+            dma((2, n)),
+            dma((2, n)),
         ],
         compiler_params=pltpu.CompilerParams(
             collective_id=0,
@@ -286,8 +324,8 @@
         out_shape=jax.ShapeDtypeStruct((rows, cols), jnp.float32),
         in_specs=[pl.BlockSpec(memory_space=pltpu.VMEM)] * 2,
         out_specs=pl.BlockSpec(memory_space=pl.ANY),
-        scratch_shapes=[pltpu.VMEM((rows, cols), jnp.float32), dma((chunks,))],
-        compiler_params=pltpu.CompilerParams(vmem_limit_bytes=rows * cols * 4 + 2 * 2**20),
+        scratch_shapes=[pltpu.VMEM((TAIL, CHUNK, cols), jnp.float32), dma((chunks,))],
+        compiler_params=pltpu.CompilerParams(vmem_limit_bytes=TAIL * CHUNK * cols * 4 + 2 * 2**20),
     )(product, scale)
 
 

time: 83 us -> 83.2 us (level)
  no operation moved by 1% of the time
where the time goes in v3:
time: 83.2 us; the launch traced here: 83 us
  Pallas kernels  83 us (100%)
    pallas_call x1, Pallas kernels, per_device(): pl.pallas_call(functools.partial(kernel, m, n), out_shape=[pltpu.VMEM((ro...  79.7 us
    pallas_call x1, Pallas kernels, per_device(): pl.pallas_call(finish, out_shape=jax.ShapeDtypeStruct((rows, cols), jnp.f...  3.37 us

profile of v3, /device:TPU:0, one launch (start us, length us, event | category | flops | bytes accessed | tf_op | source)
XLA Modules:
  0.0 83.0 jit_solution(124989497897852258)
XLA Ops:
  0.0 79.7 %shard_map.28 = (f32[1024,2048]{1,0:T(8,128)S(1)}, f32[8,128]{1,0:T(8,128)S(1)}) custom-call(bf16[1024,512]{1,0:T(8,128)(2,1)} %left.1, bf16[256,2048]{1,0:T(8,128)(2,1)} %right.1), custom_call_target="tpu_custom_call" | custom-call | tf_op jit(solution)/shard_map/pallas_call | solution.py:293
  79.7 3.4 %shard_map.29 = f32[1024,2048]{1,0:T(8,128)} custom-call(f32[1024,2048]{1,0:T(8,128)S(1)} %get-tuple-element.7.product, f32[8,128]{1,0:T(8,128)S(1)} %get-tuple-element.8.scale), custom_call_target="tpu_custom_call" | custom-call | tf_op jit(solution)/shard_map/pallas_call | solution.py:322
